TPU v7x, 32 devices: a whole 2x2x4 slice. The times are simulated.
32 devices in a mesh: dp: 8 (over z, x), sub: 4 (over y, core).
Axes of the slice: x: 2, y: 2, z: 4, core: 2. Of those that a mesh axis runs over, the one named last changes fastest.
Arguments:
- block_in: bfloat16 [32, 322, 1152], P(('dp', 'sub')), may hold values from -6 to 6
- long_skip: bfloat16 [32, 322, 1152], P(('dp', 'sub')), may hold values from -6 to 6
- lengths: int32 [32], P(('dp', 'sub')), may hold values from 192 to 320, as said below
- grad_out: bfloat16 [32, 322, 1152], P(('dp', 'sub')), may hold values from -6 to 6
- w_skip: bfloat16 [2654208], P(('dp', 'sub')), may hold values from -0.125 to 0.125
- w_qkv: bfloat16 [3981312], P(('dp', 'sub')), may hold values from -0.1875 to 0.1875
- w_out: bfloat16 [1327104], P(('dp', 'sub')), may hold values from -1.5 to 1.5
- w_up: bfloat16 [5308416], P(('dp', 'sub')), may hold values from -0.1875 to 0.1875
- w_down: bfloat16 [5308416], P(('dp', 'sub')), may hold values from -0.09375 to 0.09375
- norm_gains: float32 [2, 1152], replicated, may hold values from 0.5 to 1.5
- biases: float32 [9, 1152], replicated, may hold values from -3 to 3
Outputs:
- layer_out: bfloat16 [32, 322, 1152], P(('dp', 'sub'))
- grad_in: bfloat16 [32, 322, 1152], P(('dp', 'sub'))
- grad_skip: bfloat16 [32, 322, 1152], P(('dp', 'sub'))
- grad_w_skip: float32 [2654208], P(('dp', 'sub'))
- grad_w_qkv: float32 [3981312], P(('dp', 'sub'))
- grad_w_out: float32 [1327104], P(('dp', 'sub'))
- grad_w_up: float32 [5308416], P(('dp', 'sub'))
- grad_w_down: float32 [5308416], P(('dp', 'sub'))
- grad_gains: float32 [2, 1152], replicated
- grad_biases: float32 [9, 1152], replicated
Inputs may be any that keep to these rules, and one draw needn't show every extreme that they name: In each item, slots 0 and 1 hold its time and class tokens, slots 2 to lengths + 1 hold its patches, and the rest is padding; in every draw at least one item has 320 patches and one has 192.
All inputs are finite; a program needn't handle non-finite values.
Results may differ from a plain program's by a relative error of at most 0.014.
Values may be sent and summed in bfloat16 or wider, within the bound.
A program may use at most 320 MiB of HBM per device.

v0:
```python
import jax
import jax.numpy as jnp
from jax import lax
from jax.sharding import PartitionSpec as P

HEADS = 16
HD = 72
FF = 4608
norm_epsilon = 1e-05
masked_score = -1e30


def product(left_side, right_side):
    return jnp.dot(left_side, right_side, preferred_element_type=jnp.float32)


def cross_rows(left_side, right_side):
    return lax.dot_general(
        left_side, right_side, (((0,), (0,)), ((), ())), preferred_element_type=jnp.float32
    )


def cross_cols(left_side, right_side):
    return lax.dot_general(
        left_side, right_side, (((1,), (1,)), ((), ())), preferred_element_type=jnp.float32
    )


def flat_rows(left_side, right_side):
    block = cross_rows(left_side, right_side).reshape(-1)
    return block


def norm_forward(stream, gain_row, shift_row):
    centred = stream - jnp.mean(stream, -1, keepdims=True)
    inverse = lax.rsqrt(jnp.mean(centred * centred, -1, keepdims=True) + norm_epsilon)
    normal = centred * inverse
    return (normal * gain_row + shift_row, normal, inverse)


def norm_backward(incoming, normal, inverse, gain_row):
    grad_gain = jnp.sum(incoming * normal, 0)
    grad_shift = jnp.sum(incoming, 0)
    scaled = incoming * gain_row
    centred = scaled - jnp.mean(scaled, -1, keepdims=True)
    grad_value = inverse * (centred - normal * jnp.mean(scaled * normal, -1, keepdims=True))
    return (grad_value, grad_gain, grad_shift)


def gelu_slope(hidden):
    cumulative = 0.5 * (1.0 + lax.erf(hidden * 0.5**0.5))
    density = jnp.exp(-0.5 * hidden * hidden) * (2.0 * jnp.pi) ** (-0.5)
    return cumulative + hidden * density


def attention_shares(queries, key_rows, key_valid, score_scale):
    scores = (
        jnp.einsum("ishd,ithd->ihst", queries, key_rows, preferred_element_type=jnp.float32)
        * score_scale
    )
    scores = jnp.where(key_valid[:, None, None, :], scores, masked_score)
    highest = jnp.max(scores, -1, keepdims=True)
    raised = jnp.exp(scores - highest)
    return raised / jnp.sum(raised, -1, keepdims=True)


def on_device(
    block_in, long_skip, lengths, grad_out, w_skip, w_qkv, w_out, w_up, w_down, norm_gains, biases
):
    item_count, slot_count, model_width = block_in.shape
    row_count = item_count * slot_count
    head_count = HEADS
    head_size = HD
    hidden_width = FF
    score_scale = HD ** (-0.5)
    key_valid = jnp.arange(slot_count, dtype=jnp.int32)[None, :] < lengths[:, None] + 2
    skip_full = lax.all_gather(w_skip, ("dp", "sub"), axis=0, tiled=True).reshape(
        2 * model_width, model_width
    )
    joined = jnp.concatenate([block_in, long_skip], -1).reshape(row_count, 2 * model_width)
    stream_one = product(joined, skip_full) + biases[0]
    normed, normal_one, inverse_one = norm_forward(stream_one, norm_gains[0], biases[1])
    normed_low = normed.astype(jnp.bfloat16)
    qkv_flat, out_flat = (
        lax.all_gather(w_qkv, ("dp", "sub"), axis=0, tiled=True),
        lax.all_gather(w_out, ("dp", "sub"), axis=0, tiled=True),
    )
    qkv_full = qkv_flat.reshape(model_width, 3 * model_width)
    out_full = out_flat.reshape(model_width, model_width)
    triple = product(normed_low, qkv_full).astype(jnp.bfloat16)
    triple = triple.reshape(item_count, slot_count, 3, head_count, head_size)
    queries = triple[:, :, 0]
    key_rows = triple[:, :, 1]
    values = triple[:, :, 2]
    shares = attention_shares(queries, key_rows, key_valid, score_scale)
    shares_low = shares.astype(jnp.bfloat16)
    mixture = jnp.einsum("ihst,ithd->ishd", shares_low, values, preferred_element_type=jnp.float32)
    mixture_low = mixture.reshape(row_count, model_width).astype(jnp.bfloat16)
    stream_two = stream_one + (product(mixture_low, out_full) + biases[2])
    up_flat, down_flat = (
        lax.all_gather(w_up, ("dp", "sub"), axis=0, tiled=True),
        lax.all_gather(w_down, ("dp", "sub"), axis=0, tiled=True),
    )
    up_full = up_flat.reshape(model_width, hidden_width)
    down_full = down_flat.reshape(hidden_width, model_width)
    normed_two, normal_two, inverse_two = norm_forward(stream_two, norm_gains[1], biases[3])
    normed_two_low = normed_two.astype(jnp.bfloat16)
    hidden = product(normed_two_low, up_full) + biases[4:8].reshape(hidden_width)
    active_low = jax.nn.gelu(hidden, approximate=False).astype(jnp.bfloat16)
    result = stream_two + (product(active_low, down_full) + biases[8])
    layer_out = result.astype(jnp.bfloat16).reshape(item_count, slot_count, model_width)
    row_mask = key_valid.reshape(row_count, 1).astype(jnp.float32)
    start_grad = grad_out.reshape(row_count, model_width).astype(jnp.float32) * row_mask
    up_again, down_again = (
        lax.all_gather(w_up, ("dp", "sub"), axis=0, tiled=True),
        lax.all_gather(w_down, ("dp", "sub"), axis=0, tiled=True),
    )
    up_back = up_again.reshape(model_width, hidden_width)
    down_back = down_again.reshape(hidden_width, model_width)
    grad_branch = start_grad.astype(jnp.bfloat16)
    bias_down = jnp.sum(grad_branch.astype(jnp.float32), 0)
    part_down = lax.psum_scatter(
        flat_rows(active_low, grad_branch), ("dp", "sub"), scatter_dimension=0, tiled=True
    )
    grad_active = cross_cols(grad_branch, down_back)
    grad_hidden = (grad_active * gelu_slope(hidden)).astype(jnp.bfloat16)
    bias_up = jnp.sum(grad_hidden.astype(jnp.float32), 0)
    part_up = lax.psum_scatter(
        flat_rows(normed_two_low, grad_hidden), ("dp", "sub"), scatter_dimension=0, tiled=True
    )
    grad_normed_two = cross_cols(grad_hidden, up_back)
    local_two, gain_two, shift_two = norm_backward(
        grad_normed_two, normal_two, inverse_two, norm_gains[1]
    )
    grad_two = start_grad + local_two
    qkv_again, out_again = (
        lax.all_gather(w_qkv, ("dp", "sub"), axis=0, tiled=True),
        lax.all_gather(w_out, ("dp", "sub"), axis=0, tiled=True),
    )
    qkv_back = qkv_again.reshape(model_width, 3 * model_width)
    out_back = out_again.reshape(model_width, model_width)
    grad_attn = grad_two.astype(jnp.bfloat16)
    bias_out = jnp.sum(grad_attn.astype(jnp.float32), 0)
    part_out = lax.psum_scatter(
        flat_rows(mixture_low, grad_attn), ("dp", "sub"), scatter_dimension=0, tiled=True
    )
    grad_mixture = cross_cols(grad_attn, out_back).astype(jnp.bfloat16)
    grad_mixture = grad_mixture.reshape(item_count, slot_count, head_count, head_size)
    grad_shares = jnp.einsum(
        "ishd,ithd->ihst", grad_mixture, values, preferred_element_type=jnp.float32
    )
    grad_scores = shares * (grad_shares - jnp.sum(shares * grad_shares, -1, keepdims=True))
    grad_scores_low = grad_scores.astype(jnp.bfloat16)
    grad_queries = (
        jnp.einsum("ihst,ithd->ishd", grad_scores_low, key_rows, preferred_element_type=jnp.float32)
        * score_scale
    )
    grad_keys = (
        jnp.einsum("ihst,ishd->ithd", grad_scores_low, queries, preferred_element_type=jnp.float32)
        * score_scale
    )
    grad_values = jnp.einsum(
        "ihst,ishd->ithd", shares_low, grad_mixture, preferred_element_type=jnp.float32
    )
    grad_triple = jnp.stack([grad_queries, grad_keys, grad_values], 2).astype(jnp.bfloat16)
    grad_triple = grad_triple.reshape(row_count, 3 * model_width)
    part_qkv = lax.psum_scatter(
        flat_rows(normed_low, grad_triple), ("dp", "sub"), scatter_dimension=0, tiled=True
    )
    grad_normed = cross_cols(grad_triple, qkv_back)
    local_one, gain_one, shift_one = norm_backward(
        grad_normed, normal_one, inverse_one, norm_gains[0]
    )
    grad_one = (grad_two + local_one).astype(jnp.bfloat16)
    skip_back = lax.all_gather(w_skip, ("dp", "sub"), axis=0, tiled=True).reshape(
        2 * model_width, model_width
    )
    bias_skip = jnp.sum(grad_one.astype(jnp.float32), 0)
    part_skip = lax.psum_scatter(
        flat_rows(joined, grad_one), ("dp", "sub"), scatter_dimension=0, tiled=True
    )
    grad_joined = cross_cols(grad_one, skip_back).reshape(item_count, slot_count, 2 * model_width)
    grad_in = grad_joined[:, :, :model_width].astype(jnp.bfloat16)
    grad_skip = grad_joined[:, :, model_width:].astype(jnp.bfloat16)
    gains_part = jnp.stack([gain_one, gain_two], 0)
    biases_part = jnp.concatenate(
        [
            jnp.stack([bias_skip, shift_one, bias_out, shift_two], 0),
            bias_up.reshape(4, model_width),
            bias_down[None, :],
        ],
        0,
    )
    grad_gains, grad_biases = lax.psum((gains_part, biases_part), ("dp", "sub"))
    return (
        layer_out,
        grad_in,
        grad_skip,
        part_skip,
        part_qkv,
        part_out,
        part_up,
        part_down,
        grad_gains,
        grad_biases,
    )


def solution(mesh):
    placed = (
        P(("dp", "sub"), None, None),
        P(("dp", "sub"), None, None),
        P(("dp", "sub")),
        P(("dp", "sub"), None, None),
        P(("dp", "sub")),
        P(("dp", "sub")),
        P(("dp", "sub")),
        P(("dp", "sub")),
        P(("dp", "sub")),
        P(),
        P(),
    )
    return jax.shard_map(
        on_device,
        mesh=mesh,
        in_specs=placed,
        out_specs=(
            P(("dp", "sub"), None, None),
            P(("dp", "sub"), None, None),
            P(("dp", "sub"), None, None),
            P(("dp", "sub")),
            P(("dp", "sub")),
            P(("dp", "sub")),
            P(("dp", "sub")),
            P(("dp", "sub")),
            P(),
            P(),
        ),
        check_vma=False,
    )
```

profile of v0, /device:TPU:0, one launch (start us, length us, event | category | flops | bytes accessed | tf_op | source)
XLA Modules:
  0.0 1773.4 jit_solution(16730782300148881002)
XLA Ops:
  16.8 62.9 %all-gather.16.cloned.1.call-done = bf16[32,1,41472]{2,1,0:T(2,128)(2,1)} async-done(((bf16[1,1,41472]{2,1,0:T(2,128)(2,1)}), bf16[32,1,41472]{2,1,0:T(2,128)(2,1)}) %all-gather.16.cloned.1.call-update) | async-done | bytes 2654224 | tf_op jit(solution)/shard_map/all_gather | solution.py:86
  79.7 47.1 %reduce.10 = bf16[32,41472]{1,0:T(8,128)(2,1)S(1)} reduce(bf16[32,1,41472]{2,1,0:T(2,128)(2,1)} %all-gather.16.cloned.1.call-done, bf16[]{:T(256)} %constant.109), dimensions={1}, to_apply=%all-gather.1.reduce_sub_computation | reduce | bytes 5308418 | tf_op jit(solution)/shard_map/all_gather | solution.py:86
  131.8 14.8 all-gather.8.cloned.1.call-done
  146.6 10.8 reshape.280
  162.6 96.6 %all-gather.14.cloned.1.call-done = bf16[32,1,124416]{2,1,0:T(2,128)(2,1)} async-done(((bf16[1,1,124416]{2,1,0:T(2,128)(2,1)}), bf16[32,1,124416]{2,1,0:T(2,128)(2,1)}) %all-gather.14.cloned.1.call-update) | async-done | bytes 7962640 | tf_op jit(solution)/shard_map/all_gather | solution.py:85
  259.2 167.7 %reduce.9 = bf16[32,124416]{1,0:T(8,128)(2,1)} reduce(bf16[32,1,124416]{2,1,0:T(2,128)(2,1)} %all-gather.14.cloned.1.call-done, bf16[]{:T(256)} %constant.109), dimensions={1}, to_apply=%all-gather.reduce_sub_computation | reduce | bytes 15925250 | tf_op jit(solution)/shard_map/all_gather | solution.py:85
  426.9 14.8 reshape.281
  441.7 8.0 convolution_convert_fusion
  467.5 19.1 %reshape.287 = bf16[1152,4608]{1,0:T(8,128)(2,1)} reshape(bf16[5308416]{0:T(1024)(128)(2,1)} %all-gather.10.cloned.1.call-done) | data formatting | bytes 21233664 | tf_op jit(solution)/shard_map/reshape | solution.py:104
  486.5 20.9 %fusion.5 = (bf16[322,4608]{1,0:T(8,128)(2,1)}, f32[322,4608]{1,0:T(8,128)}) fusion(f32[4608]{0:T(1024)S(1)} %add.128, bf16[1152,4608]{1,0:T(8,128)(2,1)} %reshape.287, f32[322,1152]{1,0:T(8,128)S(1)} %get-tuple-element.44, f32[1152]{0:T(1024)S(1)} %get-tuple-element.19, f32[1152]{0:T(1024)S(1)} %get-tuple-element.23, f32[322]{0:T(512)S(1)} %add_rsqrt_fusion, ...), kind=kOutput, calls=%fused_computation.13 | convolution fusion | flops 3518403840 | bytes 21033488 | tf_op jit(solution)/shard_map/dot_general | solution.py:14
  507.5 20.4 %reshape.288 = bf16[4608,1152]{1,0:T(8,128)(2,1)} reshape(bf16[5308416]{0:T(1024)(128)(2,1)} %all-gather.12.cloned.1.call-done) | data formatting | bytes 21233664 | tf_op jit(solution)/shard_map/reshape | solution.py:105
  527.8 8.4 convert_reduce_fusion
  536.3 9.5 multiply_reduce_fusion.1
  558.5 8.3 multiply_reduce_fusion
  583.2 8.6 fusion.55
  595.7 10.5 fusion.56
  613.5 11.2 reshape.292
  624.6 16.7 reshape.293
  647.9 20.9 %reshape.295 = f32[5308416]{0:T(1024)} reshape(f32[1152,4608]{1,0:T(8,128)} %fusion.56) | data formatting | bytes 42467328 | tf_op jit(solution)/shard_map/reshape | solution.py:30
  668.8 13.0 fusion.45
  681.9 22.0 %reshape.296 = f32[5308416]{0:T(1024)} reshape(f32[4608,1152]{1,0:T(8,128)} %fusion.45) | data formatting | bytes 42467328 | tf_op jit(solution)/shard_map/reshape | solution.py:30
  704.1 42.0 %all-reduce.5 = (f32[2,1152]{1,0:T(2,128)}, f32[9,1152]{1,0:T(8,128)}) all-reduce(f32[2,1152]{1,0:T(2,128)S(1)} %pad_maximum_fusion, f32[9,1152]{1,0:T(8,128)S(1)} %concatenate.15), channel_id=1, replica_groups=mesh['dp'=8,'sub'=4] {'dp','sub'}, use_global_device_ids=true, to_apply=%region_18.19 | all-reduce | flops 12672 | bytes 101376 | tf_op jit(solution)/shard_map/psum | solution.py:194
  752.4 8.2 fusion.24
  760.6 996.3 %all-reduce.9.cloned.1.call-done = (f32[2654208]{0:T(1024)}, f32[3981312]{0:T(1024)}, f32[1327104]{0:T(1024)}, f32[5308416]{0:T(1024)}, f32[5308416]{0:T(1024)}) async-done(((f32[2654208]{0:T(1024)}, f32[3981312]{0:T(1024)}, f32[1327104]{0:T(1024)}, f32[5308416]{0:T(1024)}, f32[5308416]{0:T(1024)}), (f32[2654208]{0:T(1024)}, f32[3981312]{0:T(1024)}, f32[1327104]{0:T(1024)}, f32[5308416]{0:T(1024)}, ...) | async-done | bytes 74317840
  (115 shorter events, 99.1 us)
Async XLA Ops:
  7.2 72.5 %all-gather.16.cloned.1.call-start = ((), (), s32[]{:S(2)}) async-start(), calls=%async_computation.4 | async-start | bytes 5474304 | tf_op jit(solution)/shard_map/all_gather | solution.py:86
  8.9 137.7 %all-gather.8.cloned.1.call-start = ((), (), s32[]{:S(2)}) async-start(), calls=%async_computation | async-start | bytes 5474304 | tf_op jit(solution)/shard_map/all_gather | solution.py:77
  9.6 249.6 %all-gather.14.cloned.1.call-start = ((), (), s32[]{:S(2)}) async-start(), calls=%async_computation.3 | async-start | bytes 16422912 | tf_op jit(solution)/shard_map/all_gather | solution.py:85
  11.7 455.7 %all-gather.10.cloned.1.call-start = ((), (), s32[]{:S(2)}) async-start(), calls=%async_computation.1 | async-start | bytes 10948608 | tf_op jit(solution)/shard_map/all_gather | solution.py:101
  12.3 495.2 %all-gather.12.cloned.1.call-start = ((), (), s32[]{:S(2)}) async-start(), calls=%async_computation.2 | async-start | bytes 10948608 | tf_op jit(solution)/shard_map/all_gather | solution.py:102
  12.9 1744.0 %all-reduce.9.cloned.1.call-start = ((), (), s32[]{:S(2)}) async-start(), calls=%async_computation.5 | async-start | bytes 148635648
  131.8 25.6 %copy-start.16 = (bf16[1,322,1152]{2,1,0:T(8,128)(2,1)S(1)}, bf16[1,322,1152]{2,1,0:T(8,128)(2,1)}, u32[]{:S(2)}) copy-start(bf16[1,322,1152]{2,1,0:T(8,128)(2,1)} %param.12) | copy-start | bytes 2225668
  131.8 25.6 %copy-start.18 = (bf16[1,322,1152]{2,1,0:T(8,128)(2,1)S(1)}, bf16[1,322,1152]{2,1,0:T(8,128)(2,1)}, u32[]{:S(2)}) copy-start(bf16[1,322,1152]{2,1,0:T(8,128)(2,1)} %param.11) | copy-start | bytes 2225668
  461.0 4.0 copy-start.2
  461.0 4.7 copy-start.10
  465.0 2.4 copy-start.12
  536.2 9.6 copy-start.6
  536.3 9.6 copy-start.8
  552.6 5.9 copy-start.14
  573.5 5.6 slice-start
  576.2 2.3 copy-start.15
  576.2 2.9 slice-start.1
  583.2 8.6 copy-start.1
  583.2 8.6 copy-start.13
  591.8 3.9 copy-start.7
  647.9 20.9 %copy-start.9 = (bf16[1,322,1152]{2,1,0:T(8,128)(2,1)S(1)}, bf16[1,322,1152]{2,1,0:T(8,128)(2,1)}, u32[]{:S(2)}) copy-start(bf16[1,322,1152]{2,1,0:T(8,128)(2,1)} %param.14) | copy-start | bytes 2225668
  703.8 42.3 %copy-start.5 = (bf16[322,1152]{1,0:T(8,128)(2,1)S(1)}, bf16[322,1152]{1,0:T(8,128)(2,1)}, u32[]{:S(2)}) copy-start(bf16[322,1152]{1,0:T(8,128)(2,1)} %copy-done.4) | copy-start | bytes 2225668
  746.1 6.3 copy-start.3
  746.1 6.3 copy-start.20
  (5 other events, 6.9 us)
Sparse Core Ops, SparseCore 0:
  11.4 68.2 all-gather.15
  82.5 64.0 all-gather.7
  150.1 109.1 all-gather.13
  262.0 85.1 all-gather.9
  350.0 85.4 all-gather.11
  704.0 1052.8 all-reduce.8
where the time goes:
time: 1790 us; the launch traced here: 1770 us
  waiting for transfers between devices  1170 us (65%)
  other arithmetic  228 us (13%)
  local copies, waits for them, and re-layouts  176 us (10%)
  matrix products  140 us (8%)
  blocking collectives  42 us (2%)
    unnamed x7, waiting for transfers between devices  998 us
    all_gather x1, other arithmetic, on_device(): lax.all_gather(w_qkv, ('dp', 'sub'), axis=0, tiled=True)  168 us
    all_gather x1, waiting for transfers between devices, on_device(): lax.all_gather(w_qkv, ('dp', 'sub'), axis=0, tiled=True)  96.6 us
    reshape x5, local copies, waits for them, and re-layouts, flat_rows(): block = cross_rows(left_side, right_side).reshape(-1)  77.4 us
    all_gather x1, waiting for transfers between devices, on_device(): lax.all_gather(w_out, ('dp', 'sub'), axis=0, tiled=True)  62.9 us
    all_gather x1, other arithmetic, on_device(): lax.all_gather(w_out, ('dp', 'sub'), axis=0, tiled=True)  47.1 us
    dot_general x5, matrix products, product(): return jnp.dot(left_side, right_side, preferred_element_type=jnp.float32)  43.4 us
    psum x1, blocking collectives, on_device(): grad_gains, grad_biases = lax.psum((gains_part, biases_part), ('dp', 'sub'))  42 us
  transfers between devices with their start and end apart: 6, of which 4 were waited for; matrix products, arithmetic and copies ran while one was open for 19% of the time, Pallas kernels for 0%

commit v1 on v0

--- a/solution.py
+++ b/solution.py
@@ -8,6 +8,32 @@
 FF = 4608
 norm_epsilon = 1e-05
 masked_score = -1e30
+
+
+def _proceed_islands(body, where_dim):
+    body = jnp.moveaxis(body, 0, where_dim)
+    inter = body.shape
+    return body.reshape(
+        *inter[:where_dim], inter[where_dim] * inter[where_dim + 1], *inter[where_dim + 2 :]
+    )
+
+
+def read_shapes_in(in_array, bus_axis):
+    nd = lax.axis_size(bus_axis)
+    current_block = in_array[None]
+    for num in range(nd.bit_length() - 1):
+        q_next = 1 << num
+        left_arr = lax.ppermute(current_block, bus_axis, [(k0, k0 ^ q_next) for k0 in range(nd)])
+        back = jnp.stack([current_block, left_arr])
+        a_next = lax.axis_index(bus_axis)
+        carry = a_next >> num & 1
+        current_block = jnp.where(carry == 0, back, back[::-1]).reshape(-1, *in_array.shape)
+    return current_block
+
+
+def pipes_note(x_part, s0, join_dim):
+    frame_out = read_shapes_in(x_part, s0)
+    return _proceed_islands(frame_out, join_dim)
 
 
 def product(left_side, right_side):
@@ -82,7 +108,7 @@
     normed, normal_one, inverse_one = norm_forward(stream_one, norm_gains[0], biases[1])
     normed_low = normed.astype(jnp.bfloat16)
     qkv_flat, out_flat = (
-        lax.all_gather(w_qkv, ("dp", "sub"), axis=0, tiled=True),
+        pipes_note(w_qkv, ("dp", "sub"), 0),
         lax.all_gather(w_out, ("dp", "sub"), axis=0, tiled=True),
     )
     qkv_full = qkv_flat.reshape(model_width, 3 * model_width)

time: 1790 us -> 1920 us (1.073)
  waiting for transfers between devices: 1170 us -> 1260 us
  other arithmetic: 228 us -> 252 us
    ppermute x0 -> x5, waiting for transfers between devices: none -> 240 us  [read_shapes_in(): lax.ppermute(current_block, bus_axis, [(k0, k0 ^ q_next) for k0 in range(...]
    all_gather x1, waiting for transfers between devices: 96.6 us -> 23.6 us  [on_device(): lax.all_gather(w_qkv, ('dp', 'sub'), axis=0, tiled=True)]
    all_gather x1, waiting for transfers between devices: 62.9 us -> 0.01 us  [on_device(): lax.all_gather(w_out, ('dp', 'sub'), axis=0, tiled=True)]
  transfers between devices with their start and end apart: 6 -> 11, of which waited for: 4 -> 6; matrix products, arithmetic and copies ran while one was open for 19% -> 20% of each run, Pallas kernels for 0% -> 0%
where the time goes in v1:
time: 1920 us; the launch traced here: 1910 us
  waiting for transfers between devices  1260 us (66%)
  other arithmetic  252 us (13%)
  local copies, waits for them, and re-layouts  195 us (10%)
  matrix products  137 us (7%)
  blocking collectives  42 us (2%)
    unnamed x7, waiting for transfers between devices  996 us
    ppermute x5, waiting for transfers between devices, read_shapes_in(): lax.ppermute(current_block, bus_axis, [(k0, k0 ^ q_next) for k0 in range(...  240 us
    all_gather x1, other arithmetic, on_device(): lax.all_gather(w_qkv, ('dp', 'sub'), axis=0, tiled=True)  168 us
    reshape x5, local copies, waits for them, and re-layouts, flat_rows(): block = cross_rows(left_side, right_side).reshape(-1)  77.5 us
    all_gather x1, other arithmetic, on_device(): lax.all_gather(w_out, ('dp', 'sub'), axis=0, tiled=True)  47.1 us
    psum x1, blocking collectives, on_device(): grad_gains, grad_biases = lax.psum((gains_part, biases_part), ('dp', 'sub'))  42 us
    dot_general x5, matrix products, cross_rows(): lax.dot_general(left_side, right_side, (((0,), (0,)), ((), ())), preferre...  41.6 us
    dot_general x5, matrix products, product(): return jnp.dot(left_side, right_side, preferred_element_type=jnp.float32)  40.6 us
  transfers between devices with their start and end apart: 11, of which 6 were waited for; matrix products, arithmetic and copies ran while one was open for 20% of the time, Pallas kernels for 0%

profile of v1, /device:TPU:0, one launch (start us, length us, event | category | flops | bytes accessed | tf_op | source)
XLA Modules:
  0.0 1910.8 jit_solution(17106814730526405482)
XLA Ops:
  18.4 13.1 collective-permute-done.1
  36.3 26.6 %collective-permute-done.2 = bf16[4,124416]{1,0:T(4,128)(2,1)} collective-permute-done((bf16[4,124416]{1,0:T(4,128)(2,1)S(1)}, bf16[4,124416]{1,0:T(4,128)(2,1)}, u32[]{:S(2)}, u32[]{:S(2)}) %collective-permute-start.2) | collective-permute-done | bytes 995360 | tf_op jit(solution)/shard_map/ppermute | solution.py:26
  71.6 58.2 %collective-permute-done.3 = bf16[8,124416]{1,0:T(8,128)(2,1)} collective-permute-done((bf16[8,124416]{1,0:T(8,128)(2,1)}, bf16[8,124416]{1,0:T(8,128)(2,1)}, u32[]{:S(2)}, u32[]{:S(2)}) %collective-permute-start.3) | collective-permute-done | bytes 1990688 | tf_op jit(solution)/shard_map/ppermute | solution.py:26
  140.6 47.1 %reduce.9 = bf16[32,41472]{1,0:T(8,128)(2,1)S(1)} reduce(bf16[32,1,41472]{2,1,0:T(2,128)(2,1)} %all-gather.14.cloned.1.call-done, bf16[]{:T(256)} %constant.128), dimensions={1}, to_apply=%all-gather.reduce_sub_computation | reduce | bytes 5308418 | tf_op jit(solution)/shard_map/all_gather | solution.py:112
  192.6 142.0 %collective-permute-done.4 = bf16[16,124416]{1,0:T(8,128)(2,1)} collective-permute-done((bf16[16,124416]{1,0:T(8,128)(2,1)}, bf16[16,124416]{1,0:T(8,128)(2,1)}, u32[]{:S(2)}, u32[]{:S(2)}) %collective-permute-start.4) | collective-permute-done | bytes 3981344 | tf_op jit(solution)/shard_map/ppermute | solution.py:26
  343.2 14.8 reshape_reshape_reshape.3
  358.0 11.2 reshape.291
  398.5 23.6 %all-gather.16.cloned.1.call-done = bf16[32,1,124416]{2,1,0:T(2,128)(2,1)} async-done(((bf16[1,1,124416]{2,1,0:T(2,128)(2,1)}), bf16[32,1,124416]{2,1,0:T(2,128)(2,1)}) %all-gather.16.cloned.1.call-update) | async-done | bytes 7962640 | tf_op jit(solution)/shard_map/all_gather | solution.py:163
  422.1 167.8 %reduce.14 = bf16[32,124416]{1,0:T(8,128)(2,1)} reduce(bf16[32,1,124416]{2,1,0:T(2,128)(2,1)} %all-gather.16.cloned.1.call-done, bf16[]{:T(256)} %constant.128), dimensions={1}, to_apply=%all-gather.1.reduce_sub_computation | reduce | bytes 15925250 | tf_op jit(solution)/shard_map/all_gather | solution.py:163
  589.9 14.8 reshape.305
  604.8 19.1 reshape.301
  623.8 20.9 %fusion.5 = (bf16[322,4608]{1,0:T(8,128)(2,1)}, f32[322,4608]{1,0:T(8,128)}) fusion(f32[4608]{0:T(1024)S(1)} %add.136, bf16[1152,4608]{1,0:T(8,128)(2,1)} %reshape.301, f32[322,1152]{1,0:T(8,128)S(1)} %get-tuple-element.48, f32[1152]{0:T(1024)S(1)} %get-tuple-element.19, f32[1152]{0:T(1024)S(1)} %get-tuple-element.23, f32[322]{0:T(512)S(1)} %add_rsqrt_fusion, ...), kind=kOutput, calls=%fused_computation.15 | convolution fusion | flops 3518403840 | bytes 21033488 | tf_op jit(solution)/shard_map/dot_general | solution.py:40
  644.8 20.4 %reshape.302 = bf16[4608,1152]{1,0:T(8,128)(2,1)} reshape(bf16[5308416]{0:T(1024)(128)(2,1)} %all-gather.12.cloned.1.call-done) | data formatting | bytes 21233664 | tf_op jit(solution)/shard_map/reshape | solution.py:131
  665.1 8.4 convert_reduce_fusion
  673.6 9.5 multiply_reduce_fusion.1
  719.6 10.5 fusion.58
  730.8 8.6 fusion.57
  750.9 11.2 reshape.307
  762.1 16.7 reshape.308
  785.3 20.9 %reshape.310 = f32[5308416]{0:T(1024)} reshape(f32[1152,4608]{1,0:T(8,128)} %fusion.58) | data formatting | bytes 42467328 | tf_op jit(solution)/shard_map/reshape | solution.py:56
  806.3 12.8 fusion.47
  819.1 22.2 %reshape.311 = f32[5308416]{0:T(1024)} reshape(f32[4608,1152]{1,0:T(8,128)} %fusion.47) | data formatting | bytes 42467328 | tf_op jit(solution)/shard_map/reshape | solution.py:56
  841.5 42.0 %all-reduce.5 = (f32[2,1152]{1,0:T(2,128)}, f32[9,1152]{1,0:T(8,128)}) all-reduce(f32[2,1152]{1,0:T(2,128)S(1)} %pad_maximum_fusion.5, f32[9,1152]{1,0:T(8,128)S(1)} %concatenate.15), channel_id=1, replica_groups=mesh['dp'=8,'sub'=4] {'dp','sub'}, use_global_device_ids=true, to_apply=%region_18.19 | all-reduce | flops 12672 | bytes 101376 | tf_op jit(solution)/shard_map/psum | solution.py:220
  898.0 996.3 %all-reduce.9.cloned.1.call-done = (f32[2654208]{0:T(1024)}, f32[3981312]{0:T(1024)}, f32[1327104]{0:T(1024)}, f32[5308416]{0:T(1024)}, f32[5308416]{0:T(1024)}) async-done(((f32[2654208]{0:T(1024)}, f32[3981312]{0:T(1024)}, f32[1327104]{0:T(1024)}, f32[5308416]{0:T(1024)}, f32[5308416]{0:T(1024)}), (f32[2654208]{0:T(1024)}, f32[3981312]{0:T(1024)}, f32[1327104]{0:T(1024)}, f32[5308416]{0:T(1024)}, ...) | async-done | bytes 74317840
  (166 shorter events, 156.3 us)
Async XLA Ops:
  7.2 133.4 %all-gather.14.cloned.1.call-start = ((), (), s32[]{:S(2)}) async-start(), calls=%async_computation.3 | async-start | bytes 5474304 | tf_op jit(solution)/shard_map/all_gather | solution.py:112
  8.4 3.5 collective-permute-start
  10.7 347.3 %all-gather.8.cloned.1.call-start = ((), (), s32[]{:S(2)}) async-start(), calls=%async_computation | async-start | bytes 5474304 | tf_op jit(solution)/shard_map/all_gather | solution.py:103
  11.9 21.7 %copy-start.5 = (bf16[1,1,124416]{2,1,0:T(2,128)(2,1)}, bf16[1,1,124416]{2,1,0:T(2,128)(2,1)S(1)}, u32[]{:S(2)}) copy-start(bf16[1,1,124416]{2,1,0:T(2,128)(2,1)S(1)} %stack_broadcast_in_dim.3) | copy-start | bytes 746500
  15.7 15.8 collective-permute-start.1
  18.3 403.8 %all-gather.16.cloned.1.call-start = ((), (), s32[]{:S(2)}) async-start(), calls=%async_computation.4 | async-start | bytes 16422912 | tf_op jit(solution)/shard_map/all_gather | solution.py:163
  34.1 28.9 %collective-permute-start.2 = (bf16[4,124416]{1,0:T(4,128)(2,1)S(1)}, bf16[4,124416]{1,0:T(4,128)(2,1)}, u32[]{:S(2)}, u32[]{:S(2)}) collective-permute-start(bf16[4,124416]{1,0:T(4,128)(2,1)S(1)} %reshape.293), channel_id=1, source_target_pairs={{0,4},{1,5},{2,6},{3,7},{4,0},{5,1},{6,2},{7,3},{8,12},{9,13},{10,... | collective-permute-start | bytes 2985992 | tf_op jit(solution)/shard_map/ppermute | solution.py:26
  35.9 568.9 %all-gather.10.cloned.1.call-start = ((), (), s32[]{:S(2)}) async-start(), calls=%async_computation.1 | async-start | bytes 10948608 | tf_op jit(solution)/shard_map/all_gather | solution.py:127
  68.2 61.7 %collective-permute-start.3 = (bf16[8,124416]{1,0:T(8,128)(2,1)}, bf16[8,124416]{1,0:T(8,128)(2,1)}, u32[]{:S(2)}, u32[]{:S(2)}) collective-permute-start(bf16[8,124416]{1,0:T(8,128)(2,1)} %reshape.294), channel_id=1, source_target_pairs={{0,8},{1,9},{2,10},{3,11},{4,12},{5,13},{6,14},{7,15},{8,0},{9,1},... | collective-permute-start | bytes 5971976 | tf_op jit(solution)/shard_map/ppermute | solution.py:26
  69.8 575.0 %all-gather.12.cloned.1.call-start = ((), (), s32[]{:S(2)}) async-start(), calls=%async_computation.2 | async-start | bytes 10948608 | tf_op jit(solution)/shard_map/all_gather | solution.py:128
  132.4 7.5 copy-start.31
  136.2 198.4 %collective-permute-start.4 = (bf16[16,124416]{1,0:T(8,128)(2,1)}, bf16[16,124416]{1,0:T(8,128)(2,1)}, u32[]{:S(2)}, u32[]{:S(2)}) collective-permute-start(bf16[16,124416]{1,0:T(8,128)(2,1)} %get-tuple-element.37), channel_id=1, source_target_pairs={{0,16},{1,17},{2,18},{3,19},{4,20},{5,21},{6,22},{7,23},{8,24},{9,... | collective-permute-start | bytes 11943944 | tf_op jit(solution)/shard_map/ppermute | solution.py:26
  138.9 1755.4 %all-reduce.9.cloned.1.call-start = ((), (), s32[]{:S(2)}) async-start(), calls=%async_computation.5 | async-start | bytes 148635648
  139.9 234.7 %copy-start.22 = (f32[1152]{0:T(1024)}, f32[1152]{0:T(1024)S(1)}, u32[]{:S(2)}) copy-start(f32[1152]{0:T(1024)S(1)} %get-tuple-element.24) | copy-start | bytes 13828
  140.6 234.1 %copy-start.24 = (f32[1152]{0:T(1024)}, f32[1152]{0:T(1024)S(1)}, u32[]{:S(2)}) copy-start(f32[1152]{0:T(1024)S(1)} %get-tuple-element.21) | copy-start | bytes 13828
  357.9 11.2 copy-start.18
  358.0 11.2 copy-start.20
  673.5 9.5 copy-start.8
  673.6 9.6 copy-start.10
  719.6 10.5 copy-start.17
  730.1 9.3 slice-start
  730.8 8.6 slice-start.1
  785.3 20.9 %copy-start.11 = (bf16[1,322,1152]{2,1,0:T(8,128)(2,1)S(1)}, bf16[1,322,1152]{2,1,0:T(8,128)(2,1)}, u32[]{:S(2)}) copy-start(bf16[1,322,1152]{2,1,0:T(8,128)(2,1)} %param.14) | copy-start | bytes 2225668
  841.2 42.2 %copy-start.7 = (bf16[322,1152]{1,0:T(8,128)(2,1)S(1)}, bf16[322,1152]{1,0:T(8,128)(2,1)}, u32[]{:S(2)}) copy-start(bf16[322,1152]{1,0:T(8,128)(2,1)} %copy-done.6) | copy-start | bytes 2225668
  (22 other events, 75.4 us)
Sparse Core Ops, SparseCore 0:
  11.4 74.9 all-gather.13
  89.2 158.8 all-gather.7
  251.6 170.5 all-gather.15
  424.9 85.1 all-gather.9
  512.8 85.4 all-gather.11
  841.4 1052.8 all-reduce.8
